TPU v7x, 32 devices: a whole 2x2x4 slice. The times are simulated.
32 devices in a mesh: group: 2 (over y), seq: 4 (over z), tensor: 4 (over x, core).
Axes of the slice: x: 2, y: 2, z: 4, core: 2. Of those that a mesh axis runs over, the one named last changes fastest.
Arguments:
- query: bfloat16 [16, 7168], P(('group', 'seq'), 'tensor'), parts along dimension 0, may hold values from -5 to 5
- key_cache: bfloat16 [32, 256, 7168], P(('group', 'seq'), None, 'tensor'), parts along dimension 0, may hold values from -5 to 5
- value_cache: bfloat16 [32, 256, 7168], P(('group', 'seq'), None, 'tensor'), parts along dimension 0, may hold values from -6 to 6
- alibi_slopes: float32 [56], P('tensor'), may hold values from 0 to 1, as said below
- block_seq: int32 [32], P(('group', 'seq')), parts along dimension 0, may hold values from 0 to 7, as said below
- block_pos: int32 [32], P(('group', 'seq')), parts along dimension 0, may hold values from 0 to 2, as said below
- lengths: int32 [16], P('group'), parts along dimension 0, may hold values from 1 to 768, as said below
- out_weight: bfloat16 [7168, 14336], P('tensor', 'seq'), may hold values from -0.5 to 0.5
Outputs:
- mixed: bfloat16 [16, 14336], P(('group', 'tensor'), 'seq'), parts along dimension 0
There are 2 independent parts, one for each index of `group`. A program takes and returns all parts, laid end to end along the dimension named above; an argument that names none is the same for every part. Nothing has to cross between parts.
Inputs may be any that keep to these rules, and one draw needn't show every extreme that they name: `block_seq`: every sequence owns at least one block and at most 3; the blocks of sequence s have block_pos 0 to n_s - 1, each once. block_pos of a block is below the number of blocks its sequence owns. `lengths`: A sequence that owns n blocks has a length above 256 * (n - 1) and at most 256 * n. `alibi_slopes`: positive slopes.
All inputs are finite; a program needn't handle non-finite values.
Results may differ from a plain program's by a relative error of at most 0.0054.
Values may be sent and summed in bfloat16 or wider, within the bound.
A program may use at most 64 MiB of HBM per device.

v0:
```python
import functools
import math

import jax
import jax.numpy as jnp
from jax import lax
from jax.experimental import pallas as pl
from jax.experimental.pallas import tpu as pltpu
from jax.sharding import PartitionSpec as P

LANES = 128
OWNER_LANE = LANES - 1


def kernel(
    seq_size, tensor_size, groups, chunks,
    block_seq_in, block_pos_in, lengths_in, slopes_in, query, keys, values, weight,
    out,
    block_seq, block_pos, lengths, slopes,
    q_all, k_buf, v_buf, w_buf, stats, accs, held, part, landed,
    small_sem, q_sem, k_sem, v_sem, w_sem,
    q_send, q_recv, s_send, s_recv, a_send, a_recv, p_send, p_recv,
):
    me = lax.axis_index("seq")
    my_rows = lax.axis_index("tensor")
    blocks, block_len, features = k_buf.shape
    heads = slopes.shape[0]
    size = features // heads
    seqs = lengths.shape[0]
    query_rows = q_all.shape[1]
    rows, width = part.shape[2:]
    scale = 1.0 / math.sqrt(size)

    barrier = pltpu.get_barrier_semaphore()
    for k in range(1, seq_size):
        pl.semaphore_signal(barrier, inc=1, device_id={"seq": lax.rem(me + k, seq_size)})
    for k in range(1, tensor_size):
        pl.semaphore_signal(
            barrier, inc=1, device_id={"tensor": lax.rem(my_rows + k, tensor_size)}
        )
    q_copy = pltpu.make_async_copy(query, q_all.at[me], q_sem)
    q_copy.start()
    small_copies = [
        pltpu.make_async_copy(source, target, small_sem.at[i])
        for i, (source, target) in enumerate(
            [
                (block_seq_in, block_seq),
                (block_pos_in, block_pos),
                (lengths_in, lengths),
                (slopes_in, slopes),
            ]
        )
    ]
    for copy in small_copies:
        copy.start()
    cache_copies = [
        pltpu.make_async_copy(cache.at[b], buffer.at[b], sem.at[b])
        for cache, buffer, sem in ((keys, k_buf, k_sem), (values, v_buf, v_sem))
        for b in range(blocks)
    ]
    spans = [(first * size, last * size) for first, last in groups]
    w_copies = [
        pltpu.make_async_copy(
            weight.at[pl.ds(low, high - low)], w_buf.at[pl.ds(low, high - low)], w_sem.at[g]
        )
        for g, (low, high) in enumerate(spans)
    ]

    q_copy.wait()
    for copy in cache_copies:
        copy.start()
    pl.semaphore_wait(barrier, seq_size + tensor_size - 2)

    def to_seq(buffer, send, recv):
        copies = [
            pltpu.make_async_remote_copy(
                src_ref=buffer.at[me],
                dst_ref=buffer.at[me],
                send_sem=send.at[k - 1],
                recv_sem=recv.at[k - 1],
                device_id={"seq": lax.rem(me + k, seq_size)},
            )
            for k in range(1, seq_size)
        ]
        for copy in copies:
            copy.start()
        return copies

    q_sends = to_seq(q_all, q_send, q_recv)

    for copy in small_copies:
        copy.wait()
    offsets = lax.broadcasted_iota(jnp.int32, (1, block_len), 1)
    stat_lane = lax.broadcasted_iota(jnp.int32, (1, LANES), 1)

    for copy in q_sends:
        copy.wait_recv()
    for copy in w_copies:
        copy.start()
    for copy in cache_copies:
        copy.wait()

    q_rows = []
    for b in range(blocks):
        owner = block_seq[b]
        near = q_all[lax.div(owner, query_rows)].astype(jnp.float32)
        which = lax.rem(owner, query_rows)
        q_row = near[:1]
        for r in range(1, query_rows):
            q_row = jnp.where(which == r, near[r : r + 1], q_row)
        q_rows.append(q_row)

    s_sends, a_sends = [], []
    for g, (first, last) in enumerate(groups):
        low, high = spans[g]
        padded = -(-(last - first) // 16) * 16
        lane = lax.broadcasted_iota(jnp.int32, (padded, high - low), 1)
        row = lax.broadcasted_iota(jnp.int32, (padded, high - low), 0)
        of_head = (lane >= row * size) & (lane < row * size + size)
        head_row = lax.broadcasted_iota(jnp.int32, (padded, LANES), 0)
        head_lane = lax.broadcasted_iota(jnp.int32, (padded, LANES), 1)
        slope = jnp.zeros((padded, LANES), jnp.float32)
        for h in range(first, last):
            slope = jnp.where(head_row == h - first, slopes[h], slope)
        slope = slope[:, :1]
        weights, inverse, stat_rows = [], [], []
        for b in range(blocks):
            owner = block_seq[b]
            length = lengths[owner]
            spread = jnp.where(of_head, q_rows[b][:, low:high], 0.0).astype(jnp.bfloat16)
            scores = lax.dot_general(
                spread,
                k_buf[b, :, low:high],
                (((1,), (1,)), ((), ())),
                preferred_element_type=jnp.float32,
            )
            placed = block_pos[b] * block_len + offsets
            live = placed < length
            distance = (length - 1 - placed).astype(jnp.float32)
            scores = jnp.where(live, scores * scale - slope * distance, -1e30)
            top = jnp.max(scores, axis=1, keepdims=True)
            weight_b = jnp.where(live, jnp.exp(scores - top), 0.0)
            total = jnp.sum(weight_b, axis=1, keepdims=True)
            weights.append(weight_b.astype(jnp.bfloat16))
            inverse.append(1.0 / total)
            stat = jnp.sum(
                jnp.where(head_row == head_lane, top + jnp.log(total), 0.0), axis=0, keepdims=True
            )
            stat_rows.append(jnp.where(stat_lane == OWNER_LANE, owner.astype(jnp.float32), stat))
        stats[g][me] = jnp.concatenate(stat_rows, axis=0)
        s_sends.append(to_seq(stats[g], s_send.at[g], s_recv.at[g]))
        acc_rows = []
        for b in range(blocks):
            summed = jnp.dot(
                weights[b], v_buf[b, :, low:high], preferred_element_type=jnp.float32
            )
            summed = summed * inverse[b]
            acc_rows.append(jnp.sum(jnp.where(of_head, summed, 0.0), axis=0, keepdims=True))
        accs[g][me] = jnp.concatenate(acc_rows, axis=0).astype(jnp.bfloat16)
        a_sends.append(to_seq(accs[g], a_send.at[g], a_recv.at[g]))

    def attention_of(g):
        for copy in s_sends[g]:
            copy.wait_recv()
        stat = stats[g][...]
        owners = stat[:, :, OWNER_LANE:]
        best = jnp.zeros_like(stat)
        masks = [owners == float(s) for s in range(seqs)]
        for s in range(seqs):
            top = jnp.max(jnp.where(masks[s], stat, -1e30), axis=(0, 1), keepdims=True)
            best = jnp.where(masks[s], top, best)
        grown = jnp.exp(stat - best)
        whole = jnp.ones_like(stat)
        for s in range(seqs):
            total = jnp.sum(jnp.where(masks[s], grown, 0.0), axis=(0, 1), keepdims=True)
            whole = jnp.where(masks[s], total, whole)
        factor = grown / whole
        seq_lane = lax.broadcasted_iota(jnp.int32, (blocks, LANES), 1).astype(jnp.float32)
        owned = jnp.concatenate(
            [jnp.where(owners[j] == seq_lane, 1.0, 0.0) for j in range(seq_size)], axis=0
        )
        owned = owned.T[:seqs].astype(jnp.bfloat16)
        first, last = groups[g]
        spread = [
            jnp.concatenate(
                [
                    jnp.broadcast_to(factor[j][:, h : h + 1], (blocks, size))
                    for h in range(last - first)
                ],
                axis=1,
            )
            for j in range(seq_size)
        ]
        for copy in a_sends[g]:
            copy.wait_recv()
        w_copies[g].wait()
        scaled = jnp.concatenate(
            [accs[g][j].astype(jnp.float32) * spread[j] for j in range(seq_size)], axis=0
        )
        upper = scaled.astype(jnp.bfloat16)
        lower = (scaled - upper.astype(jnp.float32)).astype(jnp.bfloat16)
        attention = jnp.dot(owned, upper, preferred_element_type=jnp.float32) + jnp.dot(
            owned, lower, preferred_element_type=jnp.float32
        )
        return attention.astype(jnp.bfloat16)

    for g, (low, high) in enumerate(spans[:-1]):
        attention = attention_of(g)
        product = jnp.dot(attention, w_buf[low:high], preferred_element_type=jnp.float32)
        held[...] = product if g == 0 else held[...] + product
    attention = attention_of(len(groups) - 1)
    low, high = spans[-1]

    p_sends = []

    def product_of(c):
        columns = slice(c * width, (c + 1) * width)
        product = jnp.dot(attention, w_buf[low:high, columns], preferred_element_type=jnp.float32)
        return product + held[:, columns]

    later = product_of(0)
    for c in range(chunks):
        product = later
        if c + 1 < chunks:
            later = product_of(c + 1)
        for r in range(tensor_size):
            part[r, c] = product[r * rows : (r + 1) * rows]
        sends = []
        for k in range(1, tensor_size):
            peer = lax.rem(my_rows + k, tensor_size)
            copy = pltpu.make_async_remote_copy(
                src_ref=part.at[peer, c],
                dst_ref=landed.at[k - 1, c],
                send_sem=p_send.at[k - 1, c],
                recv_sem=p_recv.at[k - 1, c],
                device_id={"tensor": peer},
            )
            copy.start()
            sends.append(copy)
        p_sends.append(sends)
    for c in range(chunks):
        total = part[my_rows, c]
        for k in range(1, tensor_size):
            p_sends[c][k - 1].wait_recv()
            total = total + landed[k - 1, c]
        out[:, c * width : (c + 1) * width] = total.astype(out.dtype)
    for sends in [q_sends] + s_sends + a_sends + p_sends:
        for copy in sends:
            copy.wait_send()


def local(seq_size, tensor_size, query, key_cache, value_cache, slopes, block_seq, block_pos, lengths, weight):
    heads = slopes.shape[0]
    blocks, block_len, features = key_cache.shape
    size = features // heads
    columns = weight.shape[1]
    chunks = max([c for c in range(1, 9) if columns % (c * 256) == 0], default=1)
    width = columns // chunks
    rows = lengths.shape[0] // tensor_size
    middle = min(heads, -(-heads // 4) * 2)
    groups = [(low, high) for low, high in ((0, middle), (middle, heads)) if high > low]
    smalls = (block_seq, block_pos, lengths, slopes)
    dma = pltpu.SemaphoreType.DMA
    return pl.pallas_call(
        functools.partial(kernel, seq_size, tensor_size, groups, chunks),
        out_shape=pltpu.VMEM((rows, columns), jnp.bfloat16),
        in_specs=[pl.BlockSpec(memory_space=pltpu.HBM)] * 8,
        out_specs=pl.BlockSpec(memory_space=pltpu.VMEM),
        scratch_shapes=[pltpu.SMEM(a.shape, a.dtype) for a in smalls]
        + [
            pltpu.VMEM((seq_size,) + query.shape, query.dtype),
            pltpu.VMEM(key_cache.shape, key_cache.dtype),
            pltpu.VMEM(value_cache.shape, value_cache.dtype),
            pltpu.VMEM(weight.shape, weight.dtype),
            [pltpu.VMEM((seq_size, blocks, LANES), jnp.float32) for _ in groups],
            [
                pltpu.VMEM((seq_size, blocks, (high - low) * size), jnp.bfloat16)
                for low, high in groups
            ],
            pltpu.VMEM((lengths.shape[0], columns), jnp.float32),
            pltpu.VMEM((tensor_size, chunks, rows, width), jnp.float32),
            pltpu.VMEM((tensor_size - 1, chunks, rows, width), jnp.float32),
            dma((4,)),
            dma,
            dma((blocks,)),
            dma((blocks,)),
            dma((len(groups),)),
        ]
        + [dma((seq_size - 1,))] * 2
        + [dma((len(groups), seq_size - 1))] * 4
        + [dma((tensor_size - 1, chunks))] * 2,
        compiler_params=pltpu.CompilerParams(
            collective_id=0, has_side_effects=True, vmem_limit_bytes=48 * 1024 * 1024
        ),
    )(
        *[
            pltpu.with_memory_space_constraint(a, pltpu.HBM)
            for a in smalls + (query, key_cache, value_cache, weight)
        ]
    )


def solution(mesh):
    placed = (
        P(("group", "seq"), "tensor"),
        P(("group", "seq"), None, "tensor"),
        P(("group", "seq"), None, "tensor"),
        P("tensor"),
        P(("group", "seq")),
        P(("group", "seq")),
        P("group"),
        P("tensor", "seq"),
    )
    return jax.shard_map(
        functools.partial(local, mesh.shape["seq"], mesh.shape["tensor"]),
        mesh=mesh,
        in_specs=placed,
        out_specs=P(("group", "tensor"), "seq"),
        check_vma=False,
    )
```

profile of v0, /device:TPU:0, one launch (start us, length us, event | category | flops | bytes accessed | tf_op | source)
XLA Modules:
  0.0 20.5 jit_solution(7092304392621512264)
XLA Ops:
  0.0 19.8 %shard_map.82 = bf16[2,3584]{1,0:T(2,128)(2,1)S(1)} custom-call(s32[4]{0:T(128)} %block_seq_in.1, s32[4]{0:T(128)} %block_pos_in.1, s32[8]{0:T(128)} %lengths_in.1, f32[14]{0:T(128)} %slopes_in.1, bf16[2,1792]{1,0:T(2,128)(2,1)} %query.1, bf16[4,256,1792]{2,1,0:T(8,128)(2,1)} %keys.1, bf16[4,256,1792]{2,1,0:T(8,128)(2,1)} %values.1, bf16[1792,3584]{1,0:T(8,128)(2,1)} %weight.1), custom_call_target="tpu_custom_call" | custom-call | tf_op jit(solution)/shard_map/pallas_call | solution.py:264
  19.9 0.6 %copy.10 = bf16[2,3584]{1,0:T(2,128)(2,1)} copy(bf16[2,3584]{1,0:T(2,128)(2,1)S(1)} %shard_map.82) | data formatting | bytes 28672
where the time goes:
time: 20.6 us; the launch traced here: 20.5 us
  Pallas kernels  19.8 us (96%)
  local copies, waits for them, and re-layouts  0.6 us (3%)
    pallas_call x1, Pallas kernels, local(): pl.pallas_call(functools.partial(kernel, seq_size, tensor_size, groups, c...  19.8 us
    unnamed x1, local copies, waits for them, and re-layouts  0.6 us

commit v1 on v0

--- a/solution.py
+++ b/solution.py
@@ -54,7 +54,7 @@
     for copy in small_copies:
         copy.start()
     cache_copies = [
-        pltpu.make_async_copy(cache.at[b], buffer.at[b], sem.at[b])
+        pltpu.make_async_copy(cache.at[b], buffer.at[b], sem)
         for cache, buffer, sem in ((keys, k_buf, k_sem), (values, v_buf, v_sem))
         for b in range(blocks)
     ]
@@ -71,34 +71,38 @@
         copy.start()
     pl.semaphore_wait(barrier, seq_size + tensor_size - 2)
 
+    stride = jnp.where(me < seq_size // 2, seq_size - 1, 1)
+
+    def drain(ref, sem):
+        pltpu.make_async_copy(ref, ref, sem).wait()
+
     def to_seq(buffer, send, recv):
         copies = [
             pltpu.make_async_remote_copy(
                 src_ref=buffer.at[me],
                 dst_ref=buffer.at[me],
-                send_sem=send.at[k - 1],
-                recv_sem=recv.at[k - 1],
-                device_id={"seq": lax.rem(me + k, seq_size)},
+                send_sem=send,
+                recv_sem=recv,
+                device_id={"seq": lax.rem(me + stride * k, seq_size)},
             )
             for k in range(1, seq_size)
         ]
         for copy in copies:
             copy.start()
-        return copies
-
-    q_sends = to_seq(q_all, q_send, q_recv)
+
+    to_seq(q_all, q_send, q_recv)
 
     for copy in small_copies:
         copy.wait()
     offsets = lax.broadcasted_iota(jnp.int32, (1, block_len), 1)
     stat_lane = lax.broadcasted_iota(jnp.int32, (1, LANES), 1)
 
-    for copy in q_sends:
-        copy.wait_recv()
+    others = pl.ds(0, seq_size - 1)
+    drain(k_buf, k_sem)
+    drain(v_buf, v_sem)
     for copy in w_copies:
         copy.start()
-    for copy in cache_copies:
-        copy.wait()
+    drain(q_all.at[others], q_recv)
 
     q_rows = []
     for b in range(blocks):
@@ -110,7 +114,6 @@
             q_row = jnp.where(which == r, near[r : r + 1], q_row)
         q_rows.append(q_row)
 
-    s_sends, a_sends = [], []
     for g, (first, last) in enumerate(groups):
         low, high = spans[g]
         padded = -(-(last - first) // 16) * 16
@@ -148,7 +151,7 @@
             )
             stat_rows.append(jnp.where(stat_lane == OWNER_LANE, owner.astype(jnp.float32), stat))
         stats[g][me] = jnp.concatenate(stat_rows, axis=0)
-        s_sends.append(to_seq(stats[g], s_send.at[g], s_recv.at[g]))
+        to_seq(stats[g], s_send.at[g], s_recv.at[g])
         acc_rows = []
         for b in range(blocks):
             summed = jnp.dot(
@@ -157,11 +160,10 @@
             summed = summed * inverse[b]
             acc_rows.append(jnp.sum(jnp.where(of_head, summed, 0.0), axis=0, keepdims=True))
         accs[g][me] = jnp.concatenate(acc_rows, axis=0).astype(jnp.bfloat16)
-        a_sends.append(to_seq(accs[g], a_send.at[g], a_recv.at[g]))
+        to_seq(accs[g], a_send.at[g], a_recv.at[g])
 
     def attention_of(g):
-        for copy in s_sends[g]:
-            copy.wait_recv()
+        drain(stats[g].at[others], s_recv.at[g])
         stat = stats[g][...]
         owners = stat[:, :, OWNER_LANE:]
         best = jnp.zeros_like(stat)
@@ -191,8 +193,7 @@
             )
             for j in range(seq_size)
         ]
-        for copy in a_sends[g]:
-            copy.wait_recv()
+        drain(accs[g].at[others], a_recv.at[g])
         w_copies[g].wait()
         scaled = jnp.concatenate(
             [accs[g][j].astype(jnp.float32) * spread[j] for j in range(seq_size)], axis=0
@@ -211,8 +212,6 @@
     attention = attention_of(len(groups) - 1)
     low, high = spans[-1]
 
-    p_sends = []
-
     def product_of(c):
         columns = slice(c * width, (c + 1) * width)
         product = jnp.dot(attention, w_buf[low:high, columns], preferred_element_type=jnp.float32)
@@ -224,29 +223,27 @@
         if c + 1 < chunks:
             later = product_of(c + 1)
         for r in range(tensor_size):
-            part[r, c] = product[r * rows : (r + 1) * rows]
-        sends = []
+            part[r, c] = product[r * rows : (r + 1) * rows].astype(part.dtype)
         for k in range(1, tensor_size):
             peer = lax.rem(my_rows + k, tensor_size)
-            copy = pltpu.make_async_remote_copy(
+            pltpu.make_async_remote_copy(
                 src_ref=part.at[peer, c],
                 dst_ref=landed.at[k - 1, c],
-                send_sem=p_send.at[k - 1, c],
-                recv_sem=p_recv.at[k - 1, c],
+                send_sem=p_send,
+                recv_sem=p_recv,
                 device_id={"tensor": peer},
-            )
-            copy.start()
-            sends.append(copy)
-        p_sends.append(sends)
+            ).start()
+    drain(landed, p_recv)
     for c in range(chunks):
-        total = part[my_rows, c]
+        total = part[my_rows, c].astype(jnp.float32)
         for k in range(1, tensor_size):
-            p_sends[c][k - 1].wait_recv()
-            total = total + landed[k - 1, c]
+            total = total + landed[k - 1, c].astype(jnp.float32)
         out[:, c * width : (c + 1) * width] = total.astype(out.dtype)
-    for sends in [q_sends] + s_sends + a_sends + p_sends:
-        for copy in sends:
-            copy.wait_send()
+    drain(q_all.at[others], q_send)
+    for g in range(len(groups)):
+        drain(stats[g].at[others], s_send.at[g])
+        drain(accs[g].at[others], a_send.at[g])
+    drain(landed, p_send)
 
 
 def local(seq_size, tensor_size, query, key_cache, value_cache, slopes, block_seq, block_pos, lengths, weight):
@@ -278,17 +275,17 @@
                 for low, high in groups
             ],
             pltpu.VMEM((lengths.shape[0], columns), jnp.float32),
-            pltpu.VMEM((tensor_size, chunks, rows, width), jnp.float32),
-            pltpu.VMEM((tensor_size - 1, chunks, rows, width), jnp.float32),
+            pltpu.VMEM((tensor_size, chunks, rows, width), jnp.bfloat16),
+            pltpu.VMEM((tensor_size - 1, chunks, rows, width), jnp.bfloat16),
             dma((4,)),
             dma,
-            dma((blocks,)),
-            dma((blocks,)),
+            dma,
+            dma,
             dma((len(groups),)),
         ]
-        + [dma((seq_size - 1,))] * 2
-        + [dma((len(groups), seq_size - 1))] * 4
-        + [dma((tensor_size - 1, chunks))] * 2,
+        + [dma] * 2
+        + [dma((len(groups),))] * 4
+        + [dma] * 2,
         compiler_params=pltpu.CompilerParams(
             collective_id=0, has_side_effects=True, vmem_limit_bytes=48 * 1024 * 1024
         ),

time: 20.6 us -> 19.8 us (0.961)
  Pallas kernels: 19.8 us -> 19 us
    pallas_call x1, Pallas kernels: 19.8 us -> 19 us  [local(): pl.pallas_call(functools.partial(kernel, seq_size, tensor_size, groups, c...]
where the time goes in v1:
time: 19.8 us; the launch traced here: 19.6 us
  Pallas kernels  19 us (96%)
  local copies, waits for them, and re-layouts  0.6 us (3%)
    pallas_call x1, Pallas kernels, local(): pl.pallas_call(functools.partial(kernel, seq_size, tensor_size, groups, c...  19 us
    unnamed x1, local copies, waits for them, and re-layouts  0.6 us

profile of v1, /device:TPU:0, one launch (start us, length us, event | category | flops | bytes accessed | tf_op | source)
XLA Modules:
  0.0 19.6 jit_solution(10324461761325684395)
XLA Ops:
  0.0 19.0 %shard_map.82 = bf16[2,3584]{1,0:T(2,128)(2,1)S(1)} custom-call(s32[4]{0:T(128)} %block_seq_in.1, s32[4]{0:T(128)} %block_pos_in.1, s32[8]{0:T(128)} %lengths_in.1, f32[14]{0:T(128)} %slopes_in.1, bf16[2,1792]{1,0:T(2,128)(2,1)} %query.1, bf16[4,256,1792]{2,1,0:T(8,128)(2,1)} %keys.1, bf16[4,256,1792]{2,1,0:T(8,128)(2,1)} %values.1, bf16[1792,3584]{1,0:T(8,128)(2,1)} %weight.1), custom_call_target="tpu_custom_call" | custom-call | tf_op jit(solution)/shard_map/pallas_call | solution.py:261
  19.0 0.6 %copy.10 = bf16[2,3584]{1,0:T(2,128)(2,1)} copy(bf16[2,3584]{1,0:T(2,128)(2,1)S(1)} %shard_map.82) | data formatting | bytes 28672

commit v2 on v1

--- a/solution.py
+++ b/solution.py
@@ -17,7 +17,7 @@
     block_seq_in, block_pos_in, lengths_in, slopes_in, query, keys, values, weight,
     out,
     block_seq, block_pos, lengths, slopes,
-    q_all, k_buf, v_buf, w_buf, stats, accs, held, part, landed,
+    q_all, k_buf, kt_buf, v_buf, w_buf, stats, accs, held, part, landed,
     small_sem, q_sem, k_sem, v_sem, w_sem,
     q_send, q_recv, s_send, s_recv, a_send, a_recv, p_send, p_recv,
 ):
@@ -54,10 +54,8 @@
     for copy in small_copies:
         copy.start()
     cache_copies = [
-        pltpu.make_async_copy(cache.at[b], buffer.at[b], sem)
-        for cache, buffer, sem in ((keys, k_buf, k_sem), (values, v_buf, v_sem))
-        for b in range(blocks)
-    ]
+        pltpu.make_async_copy(keys.at[b], k_buf.at[b], k_sem.at[b]) for b in range(blocks)
+    ] + [pltpu.make_async_copy(values.at[b], v_buf.at[b], v_sem) for b in range(blocks)]
     spans = [(first * size, last * size) for first, last in groups]
     w_copies = [
         pltpu.make_async_copy(
@@ -98,119 +96,162 @@
     stat_lane = lax.broadcasted_iota(jnp.int32, (1, LANES), 1)
 
     others = pl.ds(0, seq_size - 1)
-    drain(k_buf, k_sem)
+    for b in range(blocks):
+        cache_copies[b].wait()
+        for low in range(0, features, size):
+            kt_buf[b, low : low + size, :] = k_buf[b, :, low : low + size].T
     drain(v_buf, v_sem)
     for copy in w_copies:
         copy.start()
     drain(q_all.at[others], q_recv)
 
-    q_rows = []
+    owners = [block_seq[b] for b in range(blocks)]
+    q_rows, live, distance = [], [], []
     for b in range(blocks):
-        owner = block_seq[b]
-        near = q_all[lax.div(owner, query_rows)].astype(jnp.float32)
-        which = lax.rem(owner, query_rows)
+        near = q_all[lax.div(owners[b], query_rows)].astype(jnp.float32)
+        which = lax.rem(owners[b], query_rows)
         q_row = near[:1]
         for r in range(1, query_rows):
             q_row = jnp.where(which == r, near[r : r + 1], q_row)
         q_rows.append(q_row)
-
-    for g, (first, last) in enumerate(groups):
+        length = lengths[owners[b]]
+        placed = block_pos[b] * block_len + offsets
+        live.append(placed < length)
+        distance.append((length - 1 - placed).astype(jnp.float32))
+
+    def masks_of(g):
         low, high = spans[g]
-        padded = -(-(last - first) // 16) * 16
+        padded = -(-(high - low) // (16 * size)) * 16
         lane = lax.broadcasted_iota(jnp.int32, (padded, high - low), 1)
         row = lax.broadcasted_iota(jnp.int32, (padded, high - low), 0)
-        of_head = (lane >= row * size) & (lane < row * size + size)
         head_row = lax.broadcasted_iota(jnp.int32, (padded, LANES), 0)
         head_lane = lax.broadcasted_iota(jnp.int32, (padded, LANES), 1)
+        first, last = groups[g]
         slope = jnp.zeros((padded, LANES), jnp.float32)
         for h in range(first, last):
             slope = jnp.where(head_row == h - first, slopes[h], slope)
-        slope = slope[:, :1]
-        weights, inverse, stat_rows = [], [], []
+        return (lane >= row * size) & (lane < row * size + size), head_row == head_lane, slope[:, :1]
+
+    masks = [masks_of(g) for g in range(len(groups))]
+
+    def scores_of(g):
+        low, high = spans[g]
+        return [
+            jnp.dot(
+                jnp.where(masks[g][0], q_rows[b][:, low:high], 0.0).astype(jnp.bfloat16),
+                kt_buf[b, low:high, :],
+                preferred_element_type=jnp.float32,
+            )
+            for b in range(blocks)
+        ]
+
+    def values_of(g, scores):
+        low, high = spans[g]
+        of_head, diagonal, slope = masks[g]
+        summed, inverse, stat_rows = [], [], []
         for b in range(blocks):
-            owner = block_seq[b]
-            length = lengths[owner]
-            spread = jnp.where(of_head, q_rows[b][:, low:high], 0.0).astype(jnp.bfloat16)
-            scores = lax.dot_general(
-                spread,
-                k_buf[b, :, low:high],
-                (((1,), (1,)), ((), ())),
-                preferred_element_type=jnp.float32,
-            )
-            placed = block_pos[b] * block_len + offsets
-            live = placed < length
-            distance = (length - 1 - placed).astype(jnp.float32)
-            scores = jnp.where(live, scores * scale - slope * distance, -1e30)
-            top = jnp.max(scores, axis=1, keepdims=True)
-            weight_b = jnp.where(live, jnp.exp(scores - top), 0.0)
+            score = jnp.where(live[b], scores[b] * scale - slope * distance[b], -1e30)
+            top = jnp.max(score, axis=1, keepdims=True)
+            weight_b = jnp.where(live[b], jnp.exp(score - top), 0.0)
+            summed.append(
+                jnp.dot(
+                    weight_b.astype(jnp.bfloat16),
+                    v_buf[b, :, low:high],
+                    preferred_element_type=jnp.float32,
+                )
+            )
             total = jnp.sum(weight_b, axis=1, keepdims=True)
-            weights.append(weight_b.astype(jnp.bfloat16))
             inverse.append(1.0 / total)
             stat = jnp.sum(
-                jnp.where(head_row == head_lane, top + jnp.log(total), 0.0), axis=0, keepdims=True
-            )
-            stat_rows.append(jnp.where(stat_lane == OWNER_LANE, owner.astype(jnp.float32), stat))
+                jnp.where(diagonal, top + jnp.log(total), 0.0), axis=0, keepdims=True
+            )
+            stat_rows.append(
+                jnp.where(stat_lane == OWNER_LANE, owners[b].astype(jnp.float32), stat)
+            )
         stats[g][me] = jnp.concatenate(stat_rows, axis=0)
         to_seq(stats[g], s_send.at[g], s_recv.at[g])
-        acc_rows = []
-        for b in range(blocks):
-            summed = jnp.dot(
-                weights[b], v_buf[b, :, low:high], preferred_element_type=jnp.float32
-            )
-            summed = summed * inverse[b]
-            acc_rows.append(jnp.sum(jnp.where(of_head, summed, 0.0), axis=0, keepdims=True))
+        acc_rows = [
+            jnp.sum(jnp.where(of_head, summed[b] * inverse[b], 0.0), axis=0, keepdims=True)
+            for b in range(blocks)
+        ]
         accs[g][me] = jnp.concatenate(acc_rows, axis=0).astype(jnp.bfloat16)
         to_seq(accs[g], a_send.at[g], a_recv.at[g])
 
+    scores = [scores_of(g) for g in range(min(2, len(groups)))]
+    for g in range(len(groups)):
+        values_of(g, scores[g])
+        if g + 2 < len(groups):
+            scores.append(scores_of(g + 2))
+
+    def joined(ref):
+        return jnp.concatenate([ref[j].astype(jnp.float32) for j in range(seq_size)], axis=0)
+
+    def factors_of(g):
+        stat = joined(stats[g])
+        owner = stat[:, OWNER_LANE:]
+        best, whole = jnp.zeros_like(stat), jnp.ones_like(stat)
+        owned = [owner == float(s) for s in range(seqs)]
+        for s in range(seqs):
+            top = jnp.max(jnp.where(owned[s], stat, -1e30), axis=0, keepdims=True)
+            best = jnp.where(owned[s], top, best)
+        grown = jnp.exp(stat - best)
+        for s in range(seqs):
+            total = jnp.sum(jnp.where(owned[s], grown, 0.0), axis=0, keepdims=True)
+            whole = jnp.where(owned[s], total, whole)
+        factor = grown / whole
+        first, last = groups[g]
+        spread = jnp.concatenate(
+            [jnp.broadcast_to(factor[:, h : h + 1], (factor.shape[0], size)) for h in range(last - first)],
+            axis=1,
+        )
+        return spread, owner
+
     def attention_of(g):
+        spread, owner = factors_of(g)
+        scaled = joined(accs[g]) * spread
+        seq_row = lax.broadcasted_iota(jnp.int32, (seqs, LANES), 0).astype(jnp.float32)
+        if seqs <= 16:
+            parts = []
+            for low in range(0, scaled.shape[1], LANES):
+                part_sum = jnp.zeros((seqs, LANES), jnp.float32)
+                for i in range(scaled.shape[0]):
+                    part_sum = part_sum + jnp.where(
+                        owner[i : i + 1] == seq_row, scaled[i : i + 1, low : low + LANES], 0.0
+                    )
+                parts.append(part_sum)
+            attention = jnp.concatenate(parts, axis=1)
+        else:
+            seq_lane = lax.broadcasted_iota(jnp.int32, (scaled.shape[0], LANES), 1)
+            owned = jnp.where(owner == seq_lane.astype(jnp.float32), 1.0, 0.0)
+            owned = owned.T[:seqs].astype(jnp.bfloat16)
+            upper = scaled.astype(jnp.bfloat16)
+            lower = (scaled - upper.astype(jnp.float32)).astype(jnp.bfloat16)
+            attention = jnp.dot(owned, upper, preferred_element_type=jnp.float32) + jnp.dot(
+                owned, lower, preferred_element_type=jnp.float32
+            )
+        return attention.astype(jnp.bfloat16)
+
+    def project(g, attention, left, right):
+        if left == right:
+            return
+        low, high = spans[g]
+        product = jnp.dot(
+            attention, w_buf[low:high, left:right], preferred_element_type=jnp.float32
+        )
+        held[:, left:right] = product if g == 0 else held[:, left:right] + product
+
+    half = chunks // 2 * width
+    columns_of = held.shape[1]
+    attention = None
+    for g, (low, high) in enumerate(spans):
         drain(stats[g].at[others], s_recv.at[g])
-        stat = stats[g][...]
-        owners = stat[:, :, OWNER_LANE:]
-        best = jnp.zeros_like(stat)
-        masks = [owners == float(s) for s in range(seqs)]
-        for s in range(seqs):
-            top = jnp.max(jnp.where(masks[s], stat, -1e30), axis=(0, 1), keepdims=True)
-            best = jnp.where(masks[s], top, best)
-        grown = jnp.exp(stat - best)
-        whole = jnp.ones_like(stat)
-        for s in range(seqs):
-            total = jnp.sum(jnp.where(masks[s], grown, 0.0), axis=(0, 1), keepdims=True)
-            whole = jnp.where(masks[s], total, whole)
-        factor = grown / whole
-        seq_lane = lax.broadcasted_iota(jnp.int32, (blocks, LANES), 1).astype(jnp.float32)
-        owned = jnp.concatenate(
-            [jnp.where(owners[j] == seq_lane, 1.0, 0.0) for j in range(seq_size)], axis=0
-        )
-        owned = owned.T[:seqs].astype(jnp.bfloat16)
-        first, last = groups[g]
-        spread = [
-            jnp.concatenate(
-                [
-                    jnp.broadcast_to(factor[j][:, h : h + 1], (blocks, size))
-                    for h in range(last - first)
-                ],
-                axis=1,
-            )
-            for j in range(seq_size)
-        ]
         drain(accs[g].at[others], a_recv.at[g])
         w_copies[g].wait()
-        scaled = jnp.concatenate(
-            [accs[g][j].astype(jnp.float32) * spread[j] for j in range(seq_size)], axis=0
-        )
-        upper = scaled.astype(jnp.bfloat16)
-        lower = (scaled - upper.astype(jnp.float32)).astype(jnp.bfloat16)
-        attention = jnp.dot(owned, upper, preferred_element_type=jnp.float32) + jnp.dot(
-            owned, lower, preferred_element_type=jnp.float32
-        )
-        return attention.astype(jnp.bfloat16)
-
-    for g, (low, high) in enumerate(spans[:-1]):
+        if g > 0:
+            project(g - 1, attention, half, columns_of)
         attention = attention_of(g)
-        product = jnp.dot(attention, w_buf[low:high], preferred_element_type=jnp.float32)
-        held[...] = product if g == 0 else held[...] + product
-    attention = attention_of(len(groups) - 1)
-    low, high = spans[-1]
+        if g + 1 < len(groups):
+            project(g, attention, 0, half)
 
     def product_of(c):
         columns = slice(c * width, (c + 1) * width)
@@ -254,8 +295,9 @@
     chunks = max([c for c in range(1, 9) if columns % (c * 256) == 0], default=1)
     width = columns // chunks
     rows = lengths.shape[0] // tensor_size
-    middle = min(heads, -(-heads // 4) * 2)
-    groups = [(low, high) for low, high in ((0, middle), (middle, heads)) if high > low]
+    outer = min(heads, -(-heads // 8) * 2)
+    bounds = (0, outer, max(outer, heads - outer), heads)
+    groups = [(low, high) for low, high in zip(bounds, bounds[1:]) if high > low]
     smalls = (block_seq, block_pos, lengths, slopes)
     dma = pltpu.SemaphoreType.DMA
     return pl.pallas_call(
@@ -267,6 +309,7 @@
         + [
             pltpu.VMEM((seq_size,) + query.shape, query.dtype),
             pltpu.VMEM(key_cache.shape, key_cache.dtype),
+            pltpu.VMEM((blocks, features, block_len), key_cache.dtype),
             pltpu.VMEM(value_cache.shape, value_cache.dtype),
             pltpu.VMEM(weight.shape, weight.dtype),
             [pltpu.VMEM((seq_size, blocks, LANES), jnp.float32) for _ in groups],
@@ -279,7 +322,7 @@
             pltpu.VMEM((tensor_size - 1, chunks, rows, width), jnp.bfloat16),
             dma((4,)),
             dma,
-            dma,
+            dma((blocks,)),
             dma,
             dma((len(groups),)),
         ]

time: 19.8 us -> 19 us (0.960)
  Pallas kernels: 19 us -> 18.2 us
    pallas_call x1, Pallas kernels: 19 us -> 18.2 us  [local(): pl.pallas_call(functools.partial(kernel, seq_size, tensor_size, groups, c...]
where the time goes in v2:
time: 19 us; the launch traced here: 18.9 us
  Pallas kernels  18.2 us (96%)
  local copies, waits for them, and re-layouts  0.6 us (3%)
    pallas_call x1, Pallas kernels, local(): pl.pallas_call(functools.partial(kernel, seq_size, tensor_size, groups, c...  18.2 us
    unnamed x1, local copies, waits for them, and re-layouts  0.6 us

profile of v2, /device:TPU:0, one launch (start us, length us, event | category | flops | bytes accessed | tf_op | source)
XLA Modules:
  0.0 18.9 jit_solution(731092243941971239)
XLA Ops:
  0.0 18.2 %shard_map.82 = bf16[2,3584]{1,0:T(2,128)(2,1)S(1)} custom-call(s32[4]{0:T(128)} %block_seq_in.1, s32[4]{0:T(128)} %block_pos_in.1, s32[8]{0:T(128)} %lengths_in.1, f32[14]{0:T(128)} %slopes_in.1, bf16[2,1792]{1,0:T(2,128)(2,1)} %query.1, bf16[4,256,1792]{2,1,0:T(8,128)(2,1)} %keys.1, bf16[4,256,1792]{2,1,0:T(8,128)(2,1)} %values.1, bf16[1792,3584]{1,0:T(8,128)(2,1)} %weight.1), custom_call_target="tpu_custom_call" | custom-call | tf_op jit(solution)/shard_map/pallas_call | solution.py:303
  18.3 0.6 %copy.10 = bf16[2,3584]{1,0:T(2,128)(2,1)} copy(bf16[2,3584]{1,0:T(2,128)(2,1)S(1)} %shard_map.82) | data formatting | bytes 28672

commit v3 on v2

--- a/solution.py
+++ b/solution.py
@@ -17,9 +17,9 @@
     block_seq_in, block_pos_in, lengths_in, slopes_in, query, keys, values, weight,
     out,
     block_seq, block_pos, lengths, slopes,
-    q_all, k_buf, kt_buf, v_buf, w_buf, stats, accs, held, part, landed,
+    q_all, q_pair, k_buf, kt_buf, v_buf, w_buf, stats, accs, held, part, landed,
     small_sem, q_sem, k_sem, v_sem, w_sem,
-    q_send, q_recv, s_send, s_recv, a_send, a_recv, p_send, p_recv,
+    q_send, q_recv, pair_send, pair_recv, s_send, s_recv, a_send, a_recv, p_send, p_recv,
 ):
     me = lax.axis_index("seq")
     my_rows = lax.axis_index("tensor")
@@ -32,8 +32,15 @@
     scale = 1.0 / math.sqrt(size)
 
     barrier = pltpu.get_barrier_semaphore()
+    paired = tensor_size % 2 == 0
+    relay = lax.rem(my_rows, 2) == 1 if paired else my_rows >= 0
+    partner = my_rows + 1 - 2 * lax.rem(my_rows, 2)
     for k in range(1, seq_size):
-        pl.semaphore_signal(barrier, inc=1, device_id={"seq": lax.rem(me + k, seq_size)})
+
+        @pl.when(relay | (me + k < seq_size))
+        def _():
+            pl.semaphore_signal(barrier, inc=1, device_id={"seq": lax.rem(me + k, seq_size)})
+
     for k in range(1, tensor_size):
         pl.semaphore_signal(
             barrier, inc=1, device_id={"tensor": lax.rem(my_rows + k, tensor_size)}
@@ -67,7 +74,7 @@
     q_copy.wait()
     for copy in cache_copies:
         copy.start()
-    pl.semaphore_wait(barrier, seq_size + tensor_size - 2)
+    pl.semaphore_wait(barrier, jnp.where(relay, seq_size - 1, me) + tensor_size - 1)
 
     stride = jnp.where(me < seq_size // 2, seq_size - 1, 1)
 
@@ -88,7 +95,42 @@
         for copy in copies:
             copy.start()
 
-    to_seq(q_all, q_send, q_recv)
+    def pair_copy(source, target, recv, where):
+        return pltpu.make_async_remote_copy(
+            src_ref=source, dst_ref=target, send_sem=pair_send, recv_sem=recv, device_id=where
+        )
+
+    if paired:
+
+        @pl.when(jnp.logical_not(relay) & (me < seq_size - 1))
+        def _():
+            pair_copy(
+                q_all.at[me], q_pair.at[me], pair_recv.at[me], {"tensor": partner}
+            ).start()
+
+        @pl.when(relay & (me < seq_size - 1))
+        def _():
+            pltpu.make_async_copy(q_pair.at[me], q_pair.at[me], pair_recv.at[me]).wait()
+            for k in range(seq_size - 1, 0, -1):
+
+                @pl.when(me + k < seq_size)
+                def _():
+                    pair_copy(
+                        q_pair.at[me], q_pair.at[me], pair_recv.at[me], {"seq": lax.rem(me + k, seq_size)}
+                    ).start()
+
+    q_copies = []
+    for k in range(1, seq_size):
+        peer = lax.rem(me + stride * k, seq_size)
+        copy = pltpu.make_async_remote_copy(
+            src_ref=q_all.at[me],
+            dst_ref=q_all.at[me],
+            send_sem=q_send.at[k - 1],
+            recv_sem=q_recv,
+            device_id={"seq": peer},
+        )
+        q_copies.append((relay | (peer < me), copy))
+        pl.when(q_copies[-1][0])(copy.start)
 
     for copy in small_copies:
         copy.wait()
@@ -103,6 +145,15 @@
     drain(v_buf, v_sem)
     for copy in w_copies:
         copy.start()
+    if paired:
+        for k in range(1, seq_size):
+
+            @pl.when(relay & (me >= k))
+            def _():
+                lower = lax.rem(me + seq_size - k, seq_size)
+                pltpu.make_async_copy(q_pair.at[lower], q_pair.at[lower], pair_recv.at[lower]).wait()
+                pair_copy(q_pair.at[lower], q_all.at[lower], q_recv, {"tensor": partner}).start()
+
     drain(q_all.at[others], q_recv)
 
     owners = [block_seq[b] for b in range(blocks)]
@@ -280,7 +331,18 @@
         for k in range(1, tensor_size):
             total = total + landed[k - 1, c].astype(jnp.float32)
         out[:, c * width : (c + 1) * width] = total.astype(out.dtype)
-    drain(q_all.at[others], q_send)
+    for sent, copy in q_copies:
+        pl.when(sent)(copy.wait_send)
+    if paired:
+
+        @pl.when(relay)
+        def _():
+            drain(q_pair.at[others], pair_send)
+
+        @pl.when(jnp.logical_not(relay) & (me < seq_size - 1))
+        def _():
+            drain(q_pair.at[0], pair_send)
+
     for g in range(len(groups)):
         drain(stats[g].at[others], s_send.at[g])
         drain(accs[g].at[others], a_send.at[g])
@@ -308,6 +370,7 @@
         scratch_shapes=[pltpu.SMEM(a.shape, a.dtype) for a in smalls]
         + [
             pltpu.VMEM((seq_size,) + query.shape, query.dtype),
+            pltpu.VMEM((seq_size,) + query.shape, query.dtype),
             pltpu.VMEM(key_cache.shape, key_cache.dtype),
             pltpu.VMEM((blocks, features, block_len), key_cache.dtype),
             pltpu.VMEM(value_cache.shape, value_cache.dtype),
@@ -326,7 +389,7 @@
             dma,
             dma((len(groups),)),
         ]
-        + [dma] * 2
+        + [dma((seq_size - 1,)), dma, dma, dma((seq_size,))]
         + [dma((len(groups),))] * 4
         + [dma] * 2,
         compiler_params=pltpu.CompilerParams(

time: 19 us -> 18.5 us (0.974)
  Pallas kernels: 18.2 us -> 17.8 us
    pallas_call x1, Pallas kernels: 18.2 us -> 17.8 us  [local(): pl.pallas_call(functools.partial(kernel, seq_size, tensor_size, groups, c...]
where the time goes in v3:
time: 18.5 us; the launch traced here: 18.4 us
  Pallas kernels  17.8 us (96%)
  local copies, waits for them, and re-layouts  0.6 us (3%)
    pallas_call x1, Pallas kernels, local(): pl.pallas_call(functools.partial(kernel, seq_size, tensor_size, groups, c...  17.8 us
    unnamed x1, local copies, waits for them, and re-layouts  0.6 us

profile of v3, /device:TPU:0, one launch (start us, length us, event | category | flops | bytes accessed | tf_op | source)
XLA Modules:
  0.0 18.4 jit_solution(16921806798726672457)
XLA Ops:
  0.0 17.8 %shard_map.82 = bf16[2,3584]{1,0:T(2,128)(2,1)S(1)} custom-call(s32[4]{0:T(128)} %block_seq_in.1, s32[4]{0:T(128)} %block_pos_in.1, s32[8]{0:T(128)} %lengths_in.1, f32[14]{0:T(128)} %slopes_in.1, bf16[2,1792]{1,0:T(2,128)(2,1)} %query.1, bf16[4,256,1792]{2,1,0:T(8,128)(2,1)} %keys.1, bf16[4,256,1792]{2,1,0:T(8,128)(2,1)} %values.1, bf16[1792,3584]{1,0:T(8,128)(2,1)} %weight.1), custom_call_target="tpu_custom_call" | custom-call | tf_op jit(solution)/shard_map/pallas_call | solution.py:365
  17.8 0.6 %copy.10 = bf16[2,3584]{1,0:T(2,128)(2,1)} copy(bf16[2,3584]{1,0:T(2,128)(2,1)S(1)} %shard_map.82) | data formatting | bytes 28672

commit v4 on v2

--- a/solution.py
+++ b/solution.py
@@ -17,9 +17,9 @@
     block_seq_in, block_pos_in, lengths_in, slopes_in, query, keys, values, weight,
     out,
     block_seq, block_pos, lengths, slopes,
-    q_all, k_buf, kt_buf, v_buf, w_buf, stats, accs, held, part, landed,
+    q_all, q_pair, k_buf, kt_buf, v_buf, w_buf, stats, accs, held, part, landed,
     small_sem, q_sem, k_sem, v_sem, w_sem,
-    q_send, q_recv, s_send, s_recv, a_send, a_recv, p_send, p_recv,
+    q_send, q_recv, pair_send, pair_recv, ready, s_send, s_recv, a_send, a_recv, p_send, p_recv,
 ):
     me = lax.axis_index("seq")
     my_rows = lax.axis_index("tensor")
@@ -32,12 +32,29 @@
     scale = 1.0 / math.sqrt(size)
 
     barrier = pltpu.get_barrier_semaphore()
-    for k in range(1, seq_size):
-        pl.semaphore_signal(barrier, inc=1, device_id={"seq": lax.rem(me + k, seq_size)})
-    for k in range(1, tensor_size):
-        pl.semaphore_signal(
-            barrier, inc=1, device_id={"tensor": lax.rem(my_rows + k, tensor_size)}
-        )
+    paired = tensor_size % 2 == 0
+    plain = lax.rem(my_rows, 2) == 0
+    partner = my_rows + 1 - 2 * lax.rem(my_rows, 2)
+    steps = range(1, seq_size)
+
+    def signal(when, **where):
+        @pl.when(when)
+        def _():
+            pl.semaphore_signal(barrier, inc=1, device_id=where)
+
+    for k in steps[::-1] if paired else ():
+        lower = lax.rem(me + seq_size - k, seq_size)
+        signal(plain & (me - k >= 1), seq=lower, tensor=partner)
+    for k in steps:
+        odd = jnp.logical_not(plain) if paired else me >= 0
+        signal(odd | (me + k < seq_size), seq=lax.rem(me + k, seq_size))
+    if paired:
+        signal(jnp.logical_not(plain) & (me >= 1), seq=lax.rem(me + seq_size - 1, seq_size), tensor=partner)
+    upper = [my_rows + k < tensor_size for k in range(1, tensor_size)]
+    peers = [lax.rem(my_rows + k, tensor_size) for k in range(1, tensor_size)]
+    for above, peer in zip(upper, peers):
+        signal(above, tensor=peer)
+
     q_copy = pltpu.make_async_copy(query, q_all.at[me], q_sem)
     q_copy.start()
     small_copies = [
@@ -67,7 +84,24 @@
     q_copy.wait()
     for copy in cache_copies:
         copy.start()
-    pl.semaphore_wait(barrier, seq_size + tensor_size - 2)
+    last = seq_size - 1
+    greeted = last
+    if paired:
+        from_plain = me + jnp.where(me < last, 1, 0)
+        greeted = jnp.where(plain, from_plain, last + jnp.where(me >= 1, last - me, 0))
+    if seq_size > 1:
+        pl.semaphore_wait(barrier, greeted + my_rows)
+    else:
+
+        @pl.when(my_rows > 0)
+        def _():
+            pl.semaphore_wait(barrier, my_rows)
+
+    for above, peer in zip(upper, peers):
+
+        @pl.when(jnp.logical_not(above))
+        def _():
+            pl.semaphore_signal(ready, inc=1, device_id={"tensor": peer})
 
     stride = jnp.where(me < seq_size // 2, seq_size - 1, 1)
 
@@ -88,23 +122,53 @@
         for copy in copies:
             copy.start()
 
-    to_seq(q_all, q_send, q_recv)
+    def q_copy_to(source, target, send, recv, where):
+        return pltpu.make_async_remote_copy(
+            src_ref=source, dst_ref=target, send_sem=send, recv_sem=recv, device_id=where
+        )
+
+    others = pl.ds(0, last)
+    q_copies = []
+
+    def send(when, copy):
+        q_copies.append((when, copy))
+        pl.when(when)(copy.start)
+
+    if paired and last:
+        following = {"seq": lax.rem(me + 1, seq_size), "tensor": partner}
+        send(plain & (me < last), q_copy_to(q_all.at[me], q_pair, pair_send.at[0], pair_recv, following))
+    for k in steps:
+        peer = lax.rem(me + stride * k, seq_size)
+        to_peer = jnp.logical_not(plain) | (peer < me) if paired else me >= 0
+        send(to_peer, q_copy_to(q_all.at[me], q_all.at[me], q_send.at[k - 1], q_recv, {"seq": peer}))
+    for copy in w_copies:
+        copy.start()
+    if paired and last:
+        relay = jnp.logical_not(plain) & (me >= 1)
+        source = lax.rem(me + last, seq_size)
+
+        @pl.when(relay)
+        def _():
+            drain(q_pair, pair_recv)
+
+        for k in range(last - 1, -1, -1):
+            target = {"seq": lax.rem(me + k, seq_size), "tensor": partner}
+            send(
+                relay & (me + k < seq_size),
+                q_copy_to(q_pair, q_all.at[source], pair_send.at[k], q_recv, target),
+            )
 
     for copy in small_copies:
         copy.wait()
     offsets = lax.broadcasted_iota(jnp.int32, (1, block_len), 1)
     stat_lane = lax.broadcasted_iota(jnp.int32, (1, LANES), 1)
 
-    others = pl.ds(0, seq_size - 1)
     for b in range(blocks):
         cache_copies[b].wait()
         for low in range(0, features, size):
             kt_buf[b, low : low + size, :] = k_buf[b, :, low : low + size].T
     drain(v_buf, v_sem)
-    for copy in w_copies:
-        copy.start()
     drain(q_all.at[others], q_recv)
-
     owners = [block_seq[b] for b in range(blocks)]
     q_rows, live, distance = [], [], []
     for b in range(blocks):
@@ -206,8 +270,7 @@
         )
         return spread, owner
 
-    def attention_of(g):
-        spread, owner = factors_of(g)
+    def attention_of(g, spread, owner):
         scaled = joined(accs[g]) * spread
         seq_row = lax.broadcasted_iota(jnp.int32, (seqs, LANES), 0).astype(jnp.float32)
         if seqs <= 16:
@@ -231,6 +294,10 @@
             )
         return attention.astype(jnp.bfloat16)
 
+    @pl.when(my_rows < tensor_size - 1)
+    def _():
+        pl.semaphore_wait(ready, tensor_size - 1 - my_rows)
+
     def project(g, attention, left, right):
         if left == right:
             return
@@ -244,12 +311,15 @@
     columns_of = held.shape[1]
     attention = None
     for g, (low, high) in enumerate(spans):
+        w_copies[g].wait()
         drain(stats[g].at[others], s_recv.at[g])
+        if g == 0:
+            factors = factors_of(g)
         drain(accs[g].at[others], a_recv.at[g])
-        w_copies[g].wait()
         if g > 0:
+            factors = factors_of(g)
             project(g - 1, attention, half, columns_of)
-        attention = attention_of(g)
+        attention = attention_of(g, *factors)
         if g + 1 < len(groups):
             project(g, attention, 0, half)
 
@@ -280,7 +350,8 @@
         for k in range(1, tensor_size):
             total = total + landed[k - 1, c].astype(jnp.float32)
         out[:, c * width : (c + 1) * width] = total.astype(out.dtype)
-    drain(q_all.at[others], q_send)
+    for sent, copy in q_copies:
+        pl.when(sent)(copy.wait_send)
     for g in range(len(groups)):
         drain(stats[g].at[others], s_send.at[g])
         drain(accs[g].at[others], a_send.at[g])
@@ -295,8 +366,7 @@
     chunks = max([c for c in range(1, 9) if columns % (c * 256) == 0], default=1)
     width = columns // chunks
     rows = lengths.shape[0] // tensor_size
-    outer = min(heads, -(-heads // 8) * 2)
-    bounds = (0, outer, max(outer, heads - outer), heads)
+    bounds = [0, max(1, heads * 3 // 7), heads]
     groups = [(low, high) for low, high in zip(bounds, bounds[1:]) if high > low]
     smalls = (block_seq, block_pos, lengths, slopes)
     dma = pltpu.SemaphoreType.DMA
@@ -308,6 +378,7 @@
         scratch_shapes=[pltpu.SMEM(a.shape, a.dtype) for a in smalls]
         + [
             pltpu.VMEM((seq_size,) + query.shape, query.dtype),
+            pltpu.VMEM(query.shape, query.dtype),
             pltpu.VMEM(key_cache.shape, key_cache.dtype),
             pltpu.VMEM((blocks, features, block_len), key_cache.dtype),
             pltpu.VMEM(value_cache.shape, value_cache.dtype),
@@ -326,7 +397,7 @@
             dma,
             dma((len(groups),)),
         ]
-        + [dma] * 2
+        + [dma((max(1, seq_size - 1),)), dma, dma((max(1, seq_size - 1),)), dma, pltpu.SemaphoreType.REGULAR]
         + [dma((len(groups),))] * 4
         + [dma] * 2,
         compiler_params=pltpu.CompilerParams(

time: 19 us -> 17.8 us (0.937)
  Pallas kernels: 18.2 us -> 17.1 us
    pallas_call x1, Pallas kernels: 18.2 us -> 17.1 us  [local(): pl.pallas_call(functools.partial(kernel, seq_size, tensor_size, groups, c...]
where the time goes in v4:
time: 17.8 us; the launch traced here: 17.7 us
  Pallas kernels  17.1 us (96%)
  local copies, waits for them, and re-layouts  0.6 us (3%)
    pallas_call x1, Pallas kernels, local(): pl.pallas_call(functools.partial(kernel, seq_size, tensor_size, groups, c...  17.1 us
    unnamed x1, local copies, waits for them, and re-layouts  0.6 us

profile of v4, /device:TPU:0, one launch (start us, length us, event | category | flops | bytes accessed | tf_op | source)
XLA Modules:
  0.0 17.7 jit_solution(674722740614198093)
XLA Ops:
  0.0 17.1 %shard_map.82 = bf16[2,3584]{1,0:T(2,128)(2,1)S(1)} custom-call(s32[4]{0:T(128)} %block_seq_in.1, s32[4]{0:T(128)} %block_pos_in.1, s32[8]{0:T(128)} %lengths_in.1, f32[14]{0:T(128)} %slopes_in.1, bf16[2,1792]{1,0:T(2,128)(2,1)} %query.1, bf16[4,256,1792]{2,1,0:T(8,128)(2,1)} %keys.1, bf16[4,256,1792]{2,1,0:T(8,128)(2,1)} %values.1, bf16[1792,3584]{1,0:T(8,128)(2,1)} %weight.1), custom_call_target="tpu_custom_call" | custom-call | tf_op jit(solution)/shard_map/pallas_call | solution.py:373
  17.1 0.6 %copy.10 = bf16[2,3584]{1,0:T(2,128)(2,1)} copy(bf16[2,3584]{1,0:T(2,128)(2,1)S(1)} %shard_map.82) | data formatting | bytes 28672

commit v5 on v4

--- a/solution.py
+++ b/solution.py
@@ -17,9 +17,9 @@
     block_seq_in, block_pos_in, lengths_in, slopes_in, query, keys, values, weight,
     out,
     block_seq, block_pos, lengths, slopes,
-    q_all, q_pair, k_buf, kt_buf, v_buf, w_buf, stats, accs, held, part, landed,
+    q_all, q_pair, k_buf, kt_buf, v_buf, w_buf, accs, held, part, landed,
     small_sem, q_sem, k_sem, v_sem, w_sem,
-    q_send, q_recv, pair_send, pair_recv, ready, s_send, s_recv, a_send, a_recv, p_send, p_recv,
+    q_send, q_recv, pair_send, pair_recv, ready, a_send, a_recv, p_send, p_recv,
 ):
     me = lax.axis_index("seq")
     my_rows = lax.axis_index("tensor")
@@ -28,9 +28,11 @@
     size = features // heads
     seqs = lengths.shape[0]
     query_rows = q_all.shape[1]
-    rows, width = part.shape[2:]
+    rows = part.shape[1]
     scale = 1.0 / math.sqrt(size)
 
+    q_copy = pltpu.make_async_copy(query, q_all.at[me], q_sem)
+    q_copy.start()
     barrier = pltpu.get_barrier_semaphore()
     paired = tensor_size % 2 == 0
     plain = lax.rem(my_rows, 2) == 0
@@ -55,8 +57,6 @@
     for above, peer in zip(upper, peers):
         signal(above, tensor=peer)
 
-    q_copy = pltpu.make_async_copy(query, q_all.at[me], q_sem)
-    q_copy.start()
     small_copies = [
         pltpu.make_async_copy(source, target, small_sem.at[i])
         for i, (source, target) in enumerate(
@@ -74,11 +74,15 @@
         pltpu.make_async_copy(keys.at[b], k_buf.at[b], k_sem.at[b]) for b in range(blocks)
     ] + [pltpu.make_async_copy(values.at[b], v_buf.at[b], v_sem) for b in range(blocks)]
     spans = [(first * size, last * size) for first, last in groups]
+    places = []
+    for low, high in spans:
+        start = places[-1].stop if places else 0
+        places.append(slice(start, start + high - low + 3 * LANES))
     w_copies = [
         pltpu.make_async_copy(
-            weight.at[pl.ds(low, high - low)], w_buf.at[pl.ds(low, high - low)], w_sem.at[g]
-        )
-        for g, (low, high) in enumerate(spans)
+            weight.at[pl.ds(low, high - low)], w_buf.at[pl.ds(low, high - low)], w_sem
+        )
+        for low, high in spans
     ]
 
     q_copy.wait()
@@ -108,11 +112,11 @@
     def drain(ref, sem):
         pltpu.make_async_copy(ref, ref, sem).wait()
 
-    def to_seq(buffer, send, recv):
+    def to_seq(buffer, where, send, recv):
         copies = [
             pltpu.make_async_remote_copy(
-                src_ref=buffer.at[me],
-                dst_ref=buffer.at[me],
+                src_ref=buffer.at[me, :, where],
+                dst_ref=buffer.at[me, :, where],
                 send_sem=send,
                 recv_sem=recv,
                 device_id={"seq": lax.rem(me + stride * k, seq_size)},
@@ -232,14 +236,19 @@
             stat_rows.append(
                 jnp.where(stat_lane == OWNER_LANE, owners[b].astype(jnp.float32), stat)
             )
-        stats[g][me] = jnp.concatenate(stat_rows, axis=0)
-        to_seq(stats[g], s_send.at[g], s_recv.at[g])
+        stat = jnp.concatenate(stat_rows, axis=0)
+        pieces = []
+        for _ in range(3):
+            pieces.append(stat.astype(jnp.bfloat16))
+            stat = stat - pieces[-1].astype(jnp.float32)
         acc_rows = [
             jnp.sum(jnp.where(of_head, summed[b] * inverse[b], 0.0), axis=0, keepdims=True)
             for b in range(blocks)
         ]
-        accs[g][me] = jnp.concatenate(acc_rows, axis=0).astype(jnp.bfloat16)
-        to_seq(accs[g], a_send.at[g], a_recv.at[g])
+        acc = jnp.concatenate(acc_rows, axis=0).astype(jnp.bfloat16)
+        where = places[g]
+        accs[me, :, where] = jnp.concatenate([acc] + pieces, axis=1)
+        to_seq(accs, where, a_send, a_recv.at[g])
 
     scores = [scores_of(g) for g in range(min(2, len(groups)))]
     for g in range(len(groups)):
@@ -247,11 +256,17 @@
         if g + 2 < len(groups):
             scores.append(scores_of(g + 2))
 
-    def joined(ref):
-        return jnp.concatenate([ref[j].astype(jnp.float32) for j in range(seq_size)], axis=0)
+    def joined(ref, low, high):
+        return jnp.concatenate(
+            [ref[j, :, low:high].astype(jnp.float32) for j in range(seq_size)], axis=0
+        )
 
     def factors_of(g):
-        stat = joined(stats[g])
+        low, high = spans[g]
+        stat = jnp.zeros((), jnp.float32)
+        for i in range(3):
+            start = places[g].start + high - low + i * LANES
+            stat = stat + joined(accs, start, start + LANES)
         owner = stat[:, OWNER_LANE:]
         best, whole = jnp.zeros_like(stat), jnp.ones_like(stat)
         owned = [owner == float(s) for s in range(seqs)]
@@ -271,7 +286,8 @@
         return spread, owner
 
     def attention_of(g, spread, owner):
-        scaled = joined(accs[g]) * spread
+        start = places[g].start
+        scaled = joined(accs, start, start + spread.shape[1]) * spread
         seq_row = lax.broadcasted_iota(jnp.int32, (seqs, LANES), 0).astype(jnp.float32)
         if seqs <= 16:
             parts = []
@@ -307,54 +323,48 @@
         )
         held[:, left:right] = product if g == 0 else held[:, left:right] + product
 
-    half = chunks // 2 * width
+    half = held.shape[1] // (2 * LANES * 2) * (LANES * 2)
     columns_of = held.shape[1]
     attention = None
     for g, (low, high) in enumerate(spans):
-        w_copies[g].wait()
-        drain(stats[g].at[others], s_recv.at[g])
         if g == 0:
-            factors = factors_of(g)
-        drain(accs[g].at[others], a_recv.at[g])
+            drain(w_buf, w_sem)
+        drain(accs.at[others, :, places[g]], a_recv.at[g])
+        factors = factors_of(g)
         if g > 0:
-            factors = factors_of(g)
             project(g - 1, attention, half, columns_of)
         attention = attention_of(g, *factors)
         if g + 1 < len(groups):
             project(g, attention, 0, half)
 
-    def product_of(c):
-        columns = slice(c * width, (c + 1) * width)
+    def product_of(columns):
         product = jnp.dot(attention, w_buf[low:high, columns], preferred_element_type=jnp.float32)
         return product + held[:, columns]
 
-    later = product_of(0)
-    for c in range(chunks):
+    later = product_of(chunks[0])
+    for c, columns in enumerate(chunks):
         product = later
-        if c + 1 < chunks:
-            later = product_of(c + 1)
+        if c + 1 < len(chunks):
+            later = product_of(chunks[c + 1])
         for r in range(tensor_size):
-            part[r, c] = product[r * rows : (r + 1) * rows].astype(part.dtype)
+            part[r, :, columns] = product[r * rows : (r + 1) * rows].astype(part.dtype)
         for k in range(1, tensor_size):
             peer = lax.rem(my_rows + k, tensor_size)
             pltpu.make_async_remote_copy(
-                src_ref=part.at[peer, c],
-                dst_ref=landed.at[k - 1, c],
+                src_ref=part.at[peer, :, columns],
+                dst_ref=landed.at[k - 1, :, columns],
                 send_sem=p_send,
                 recv_sem=p_recv,
                 device_id={"tensor": peer},
             ).start()
     drain(landed, p_recv)
-    for c in range(chunks):
-        total = part[my_rows, c].astype(jnp.float32)
-        for k in range(1, tensor_size):
-            total = total + landed[k - 1, c].astype(jnp.float32)
-        out[:, c * width : (c + 1) * width] = total.astype(out.dtype)
+    total = part[my_rows].astype(jnp.float32)
+    for k in range(1, tensor_size):
+        total = total + landed[k - 1].astype(jnp.float32)
+    out[...] = total.astype(out.dtype)
     for sent, copy in q_copies:
         pl.when(sent)(copy.wait_send)
-    for g in range(len(groups)):
-        drain(stats[g].at[others], s_send.at[g])
-        drain(accs[g].at[others], a_send.at[g])
+    drain(accs.at[others], a_send)
     drain(landed, p_send)
 
 
@@ -363,10 +373,11 @@
     blocks, block_len, features = key_cache.shape
     size = features // heads
     columns = weight.shape[1]
-    chunks = max([c for c in range(1, 9) if columns % (c * 256) == 0], default=1)
-    width = columns // chunks
+    tiles = columns // (2 * LANES)
+    cuts = [tiles * c // 4 * (2 * LANES) for c in range(4)] + [columns]
+    chunks = [slice(low, high) for low, high in zip(cuts, cuts[1:]) if high > low]
     rows = lengths.shape[0] // tensor_size
-    bounds = [0, max(1, heads * 3 // 7), heads]
+    bounds = [0, heads * 2 // 7, heads * 4 // 7, heads]
     groups = [(low, high) for low, high in zip(bounds, bounds[1:]) if high > low]
     smalls = (block_seq, block_pos, lengths, slopes)
     dma = pltpu.SemaphoreType.DMA
@@ -383,22 +394,18 @@
             pltpu.VMEM((blocks, features, block_len), key_cache.dtype),
             pltpu.VMEM(value_cache.shape, value_cache.dtype),
             pltpu.VMEM(weight.shape, weight.dtype),
-            [pltpu.VMEM((seq_size, blocks, LANES), jnp.float32) for _ in groups],
-            [
-                pltpu.VMEM((seq_size, blocks, (high - low) * size), jnp.bfloat16)
-                for low, high in groups
-            ],
+            pltpu.VMEM((seq_size, blocks, features + 3 * LANES * len(groups)), jnp.bfloat16),
             pltpu.VMEM((lengths.shape[0], columns), jnp.float32),
-            pltpu.VMEM((tensor_size, chunks, rows, width), jnp.bfloat16),
-            pltpu.VMEM((tensor_size - 1, chunks, rows, width), jnp.bfloat16),
+            pltpu.VMEM((tensor_size, rows, columns), jnp.bfloat16),
+            pltpu.VMEM((tensor_size - 1, rows, columns), jnp.bfloat16),
             dma((4,)),
             dma,
             dma((blocks,)),
             dma,
-            dma((len(groups),)),
+            dma,
         ]
         + [dma((max(1, seq_size - 1),)), dma, dma((max(1, seq_size - 1),)), dma, pltpu.SemaphoreType.REGULAR]
-        + [dma((len(groups),))] * 4
+        + [dma, dma((len(groups),))]
         + [dma] * 2,
         compiler_params=pltpu.CompilerParams(
             collective_id=0, has_side_effects=True, vmem_limit_bytes=48 * 1024 * 1024

time: 17.8 us -> 17.8 us (level)
  no operation moved by 1% of the time
where the time goes in v5:
time: 17.8 us; the launch traced here: 17.6 us
  Pallas kernels  17 us (96%)
  local copies, waits for them, and re-layouts  0.6 us (3%)
    pallas_call x1, Pallas kernels, local(): pl.pallas_call(functools.partial(kernel, seq_size, tensor_size, groups, c...  17 us
    unnamed x1, local copies, waits for them, and re-layouts  0.6 us

profile of v5, /device:TPU:0, one launch (start us, length us, event | category | flops | bytes accessed | tf_op | source)
XLA Modules:
  0.0 17.6 jit_solution(18290839487067762410)
XLA Ops:
  0.0 17.0 %shard_map.82 = bf16[2,3584]{1,0:T(2,128)(2,1)S(1)} custom-call(s32[4]{0:T(128)} %block_seq_in.1, s32[4]{0:T(128)} %block_pos_in.1, s32[8]{0:T(128)} %lengths_in.1, f32[14]{0:T(128)} %slopes_in.1, bf16[2,1792]{1,0:T(2,128)(2,1)} %query.1, bf16[4,256,1792]{2,1,0:T(8,128)(2,1)} %keys.1, bf16[4,256,1792]{2,1,0:T(8,128)(2,1)} %values.1, bf16[1792,3584]{1,0:T(8,128)(2,1)} %weight.1), custom_call_target="tpu_custom_call" | custom-call | tf_op jit(solution)/shard_map/pallas_call | solution.py:384
  17.0 0.6 %copy.10 = bf16[2,3584]{1,0:T(2,128)(2,1)} copy(bf16[2,3584]{1,0:T(2,128)(2,1)S(1)} %shard_map.82) | data formatting | bytes 28672

commit v6 on v5

--- a/solution.py
+++ b/solution.py
@@ -9,7 +9,6 @@
 from jax.sharding import PartitionSpec as P
 
 LANES = 128
-OWNER_LANE = LANES - 1
 
 
 def kernel(
@@ -77,7 +76,7 @@
     places = []
     for low, high in spans:
         start = places[-1].stop if places else 0
-        places.append(slice(start, start + high - low + 3 * LANES))
+        places.append(slice(start, start + high - low + 4 * LANES))
     w_copies = [
         pltpu.make_async_copy(
             weight.at[pl.ds(low, high - low)], w_buf.at[pl.ds(low, high - low)], w_sem
@@ -165,7 +164,6 @@
     for copy in small_copies:
         copy.wait()
     offsets = lax.broadcasted_iota(jnp.int32, (1, block_len), 1)
-    stat_lane = lax.broadcasted_iota(jnp.int32, (1, LANES), 1)
 
     for b in range(blocks):
         cache_copies[b].wait()
@@ -233,14 +231,16 @@
             stat = jnp.sum(
                 jnp.where(diagonal, top + jnp.log(total), 0.0), axis=0, keepdims=True
             )
-            stat_rows.append(
-                jnp.where(stat_lane == OWNER_LANE, owners[b].astype(jnp.float32), stat)
-            )
+            stat_rows.append(stat)
         stat = jnp.concatenate(stat_rows, axis=0)
         pieces = []
         for _ in range(3):
             pieces.append(stat.astype(jnp.bfloat16))
             stat = stat - pieces[-1].astype(jnp.float32)
+        owner_rows = [
+            jnp.broadcast_to(owners[b].astype(jnp.float32), (1, LANES)) for b in range(blocks)
+        ]
+        pieces.append(jnp.concatenate(owner_rows, axis=0).astype(jnp.bfloat16))
         acc_rows = [
             jnp.sum(jnp.where(of_head, summed[b] * inverse[b], 0.0), axis=0, keepdims=True)
             for b in range(blocks)
@@ -267,7 +267,7 @@
         for i in range(3):
             start = places[g].start + high - low + i * LANES
             stat = stat + joined(accs, start, start + LANES)
-        owner = stat[:, OWNER_LANE:]
+        owner = joined(accs, start + LANES, start + 2 * LANES)
         best, whole = jnp.zeros_like(stat), jnp.ones_like(stat)
         owned = [owner == float(s) for s in range(seqs)]
         for s in range(seqs):
@@ -394,7 +394,7 @@
             pltpu.VMEM((blocks, features, block_len), key_cache.dtype),
             pltpu.VMEM(value_cache.shape, value_cache.dtype),
             pltpu.VMEM(weight.shape, weight.dtype),
-            pltpu.VMEM((seq_size, blocks, features + 3 * LANES * len(groups)), jnp.bfloat16),
+            pltpu.VMEM((seq_size, blocks, features + 4 * LANES * len(groups)), jnp.bfloat16),
             pltpu.VMEM((lengths.shape[0], columns), jnp.float32),
             pltpu.VMEM((tensor_size, rows, columns), jnp.bfloat16),
             pltpu.VMEM((tensor_size - 1, rows, columns), jnp.bfloat16),

time: 17.8 us -> 17.7 us (level)
  no operation moved by 1% of the time
where the time goes in v6:
time: 17.7 us; the launch traced here: 17.5 us
  Pallas kernels  16.9 us (95%)
  local copies, waits for them, and re-layouts  0.6 us (3%)
    pallas_call x1, Pallas kernels, local(): pl.pallas_call(functools.partial(kernel, seq_size, tensor_size, groups, c...  16.9 us
    unnamed x1, local copies, waits for them, and re-layouts  0.6 us

profile of v6, /device:TPU:0, one launch (start us, length us, event | category | flops | bytes accessed | tf_op | source)
XLA Modules:
  0.0 17.5 jit_solution(8831405013838474135)
XLA Ops:
  0.0 16.9 %shard_map.82 = bf16[2,3584]{1,0:T(2,128)(2,1)S(1)} custom-call(s32[4]{0:T(128)} %block_seq_in.1, s32[4]{0:T(128)} %block_pos_in.1, s32[8]{0:T(128)} %lengths_in.1, f32[14]{0:T(128)} %slopes_in.1, bf16[2,1792]{1,0:T(2,128)(2,1)} %query.1, bf16[4,256,1792]{2,1,0:T(8,128)(2,1)} %keys.1, bf16[4,256,1792]{2,1,0:T(8,128)(2,1)} %values.1, bf16[1792,3584]{1,0:T(8,128)(2,1)} %weight.1), custom_call_target="tpu_custom_call" | custom-call | tf_op jit(solution)/shard_map/pallas_call | solution.py:384
  16.9 0.6 %copy.10 = bf16[2,3584]{1,0:T(2,128)(2,1)} copy(bf16[2,3584]{1,0:T(2,128)(2,1)S(1)} %shard_map.82) | data formatting | bytes 28672
